TPU v7x, 128 devices: a whole 4x4x4 slice. The times are simulated.
128 devices in a mesh: gy: 4 (over z_lo, core), gx: 32 (over z_hi, y, x).
Axes of the slice: x: 4, y: 4, z: 4 (z_hi: 2, z_lo: 2; z = z_hi * 2 + z_lo), core: 2. Of those that a mesh axis runs over, the one named last changes fastest.
Arguments:
- first_factor: bfloat16 [4096, 8192], P('gy', 'gx'), may hold values from -6 to 6
- second_factor: bfloat16 [8192, 32768], P('gy', 'gx'), may hold values from -0.0625 to 0.0625
- result_in: float32 [4096, 32768], P('gy', 'gx'), may hold values from -6 to 6
- pivot_scale: float32 [8192], replicated, may hold values from 0.25 to 1.75
Outputs:
- corrected: float32 [4096, 32768], P('gy', 'gx')
All inputs are finite; a program needn't handle non-finite values.
Results may differ from a plain program's by a relative error of at most 0.002.
Values may be sent and summed in bfloat16 or wider, within the bound.
No kernel may reach another device: no remote copies, remote signals or barrier semaphores. Data moves between devices by JAX's collectives and lax.ppermute only.
A program may use at most 128 MiB of HBM per device.

v0:
```python
import functools

import jax
import jax.numpy as jnp
from jax import lax
from jax.experimental import pallas as pl
from jax.experimental.pallas import tpu as pltpu
from jax.sharding import Mesh, PartitionSpec as P


RING = 4
WIDTH = 256


def flip_low(i):
    return i ^ 1


def flip_high(i):
    return RING - 1 - i


def exchange(block, axis, step):
    pairs = []
    for core in range(2):
        partner = flip_low if (core + step) % 2 == 0 else flip_high
        pairs += [(core * RING + i, core * RING + partner(i)) for i in range(RING)]
    return lax.ppermute(block, ("c", axis), pairs)


def joined(held, arrived):
    return jnp.concatenate([held, arrived])


def spread_line(own, axis):
    held = own
    for k in range(2):
        held = joined(held, exchange(held, axis, k))
    return held


def spread_plane(held, second):
    held = joined(held, exchange(held, second, 0))
    return held, exchange(held, second, 1)


def ring_slots(me, core):
    low, high = flip_low(me), flip_high(me)
    one = jnp.where(core == 0, low, high)
    two = jnp.where(core == 0, high, low)
    across = (me + 2) % RING
    return [me, one, two, across]


def slot_columns(slot, x_first):
    core = lax.axis_index("c")
    xs = ring_slots(lax.axis_index("x"), core)
    ys = ring_slots(lax.axis_index("y"), core)
    if x_first:
        x, y = xs[slot % RING], ys[slot // RING]
    else:
        x, y = xs[slot // RING], ys[slot % RING]
    mine = (y // 2) == core
    return ((y % 2) * RING + x + jnp.where(mine, 0, 8)) * WIDTH


def load_left(parts, left, sems):
    rows = left.shape[0] // 2
    copies = []
    for colour in range(2):
        for slot in range(16):
            source = parts[colour * 2 + slot // 8].at[slot % 8]
            columns = pl.multiple_of(slot_columns(slot, colour == 0), WIDTH)
            copies.append(
                pltpu.make_async_copy(
                    source,
                    left.at[pl.ds(colour * rows, rows), pl.ds(columns, WIDTH)],
                    sems.at[colour * 16 + slot],
                )
            )
    return copies


def load_slots(parts, left, sems):
    rows = left.shape[0] // 2
    return [
        pltpu.make_async_copy(
            parts[colour].at[slot],
            left.at[pl.ds(colour * rows, rows), pl.ds(slot * WIDTH, WIDTH)],
            sems.at[colour * 8 + slot],
        )
        for colour in range(2)
        for slot in range(8)
    ]


def product(left, right):
    return jnp.dot(left, right, preferred_element_type=jnp.float32)


def slot_product(left, mine, partner, colour, first_slot):
    rows = left.shape[0] // 2
    depth = mine.shape[0]
    total = None
    for slot in range(8):
        begin = slot_columns(first_slot + slot, colour == 0)
        here = pl.multiple_of(jnp.minimum(begin, depth - WIDTH), WIDTH)
        there = pl.multiple_of(jnp.maximum(begin - depth, 0), WIDTH)
        right = jnp.where(
            begin < depth, mine[pl.ds(here, WIDTH), :], partner[pl.ds(there, WIDTH), :]
        )
        term = product(
            left[colour * rows : (colour + 1) * rows, slot * WIDTH : (slot + 1) * WIDTH], right
        )
        total = term if total is None else total + term
    return total


def local_kernel(x0, y0, mine, partner, result_ref, out_ref, left, sems):
    @pl.when(pl.program_id(0) == 0)
    def _():
        copies = load_slots((x0, y0), left, sems)
        for copy in copies:
            copy.start()
        for copy in copies:
            copy.wait()

    rows = left.shape[0] // 2
    for colour in range(2):
        here = slice(colour * rows, (colour + 1) * rows)
        out_ref[here, :] = result_ref[here, :] - slot_product(left, mine, partner, colour, 0)


def remote_kernel(x0, x1, y0, y1, same, relayed, so_far, out_ref, rest_ref, left, sems):
    first = same.shape[0]
    depth = left.shape[1] // 2

    @pl.when(pl.program_id(0) == 0)
    def _():
        copies = load_left((x0, x1, y0, y1), left, sems)
        for copy in copies:
            copy.start()
        for copy in copies:
            copy.wait()
        rest_ref[:, : depth - first] = left[:, first:depth]
        rest_ref[:, depth - first :] = left[:, depth + first :]

    out_ref[...] = so_far[...] - (
        product(left[:, :first], same[...])
        + product(left[:, depth : depth + first], relayed[...])
    )


def final_kernel(
    x1, y1, mine, partner, rest, same, relayed, so_far, out_ref, power_ref, left, power, sems
):
    step = pl.program_id(0)
    last = same.shape[0]

    @pl.when(step == 0)
    def _():
        copies = load_slots((x1, y1), left, sems)
        for copy in copies:
            copy.start()
        power[...] = jnp.zeros_like(power)
        for copy in copies:
            copy.wait()

    rows = left.shape[0] // 2
    lanes = power.shape[1]
    for colour in range(2):
        here = slice(colour * rows, (colour + 1) * rows)
        total = slot_product(left, mine, partner, colour, 8)
        total += product(rest[here, :last], same[...]) + product(rest[here, last:], relayed[...])
        corrected = so_far[here, :] - total
        out_ref[here, :] = corrected
        squares = corrected * corrected
        for i in range(squares.shape[1] // lanes):
            power[here, :] += squares[:, i * lanes : (i + 1) * lanes]

    @pl.when(step == pl.num_programs(0) - 1)
    def _():
        for i in range(power.shape[0] // lanes):
            block = power[i * lanes : (i + 1) * lanes, :]
            power_ref[i : i + 1, :] = jnp.sum(block.T, axis=0, keepdims=True)


def scale_kernel(columns, power_ref, corrected_ref, out_ref, factor):
    lanes = power_ref.shape[-1]
    row_power = jnp.sum(power_ref[...], axis=0)
    inverse = lax.rsqrt(row_power / columns + 1e-06)
    step = pl.program_id(0)
    del step
    for i in range(inverse.shape[0]):
        factor[...] = jnp.broadcast_to(inverse[i : i + 1, :], (lanes, lanes)).T
        for j in range(out_ref.shape[1] // lanes):
            here = (slice(i * lanes, (i + 1) * lanes), slice(j * lanes, (j + 1) * lanes))
            out_ref[here] = corrected_ref[here] * factor[...]


def matmul_cost(rows, depth, columns, extra):
    return pl.CostEstimate(
        flops=2 * rows * depth * columns,
        bytes_accessed=2 * (rows * depth + depth * columns) + extra,
        transcendentals=0,
    )


ANY = pl.BlockSpec(memory_space=pl.ANY)


def shards(first_factor, second_factor, result_in, pivot_scale):
    rows, width = first_factor.shape
    depth, columns = second_factor.shape
    half = rows // 2
    tile = 256
    hi = lax.axis_index("hi")
    place = (hi * 4 + lax.axis_index("y")) * 4 + lax.axis_index("x")
    part_scale = lax.dynamic_slice_in_dim(pivot_scale, place * width, width)
    scaled = (first_factor.astype(jnp.float32) * part_scale).astype(jnp.bfloat16)

    foreign = lax.ppermute(scaled, "hi", [(0, 1), (1, 0)])

    first = depth * 3 // 4
    swap = [(0, 1), (1, 0)]
    same0 = lax.ppermute(second_factor[:first], "lo", swap)
    same1 = lax.ppermute(second_factor[first:], "lo", swap)
    partner = lax.ppermute(second_factor, "c", swap)
    relayed0 = lax.ppermute(same0, "c", swap)
    relayed1 = lax.ppermute(same1, "c", swap)

    def lines(block):
        return (spread_line(block[None, :half], "x"), spread_line(block[None, half:], "y"))

    def planes(line_x, line_y):
        return (*spread_plane(line_x, "y"), *spread_plane(line_y, "x"))

    near = hi == lax.axis_index("lo")
    native = lines(scaled)
    foreign = lines(foreign)
    remote_x0, remote_x1, remote_y0, remote_y1 = planes(
        *(jnp.where(near, f, n) for n, f in zip(native, foreign))
    )
    local_x0, local_x1, local_y0, local_y1 = planes(
        *(jnp.where(near, n, f) for n, f in zip(native, foreign))
    )

    def params(mebibytes):
        return pltpu.CompilerParams(vmem_limit_bytes=mebibytes * 2**20)

    def columns_of(array):
        return pl.BlockSpec((array.shape[0], tile), lambda j: (0, j))

    def whole(*shape):
        return pl.BlockSpec(shape, lambda j: (0,) * len(shape))

    grid = (columns // tile,)
    sums = jax.ShapeDtypeStruct((rows, columns), jnp.float32)
    tile_spec = columns_of(sums)
    eight_slots = [pltpu.VMEM((rows, 8 * WIDTH), jnp.bfloat16)]
    so_far = pl.pallas_call(
        local_kernel,
        grid=grid,
        out_shape=sums,
        in_specs=[ANY] * 2 + [columns_of(second_factor)] * 2 + [tile_spec],
        out_specs=tile_spec,
        scratch_shapes=eight_slots + [pltpu.SemaphoreType.DMA((16,))],
        compiler_params=params(16),
        cost_estimate=matmul_cost(rows, 8 * WIDTH, columns, rows * columns * 4),
        name="local",
    )(local_x0, local_y0, second_factor, partner, result_in)

    rest = 2 * (depth - first)
    so_far, left_over = pl.pallas_call(
        remote_kernel,
        grid=grid,
        out_shape=(sums, jax.ShapeDtypeStruct((rows, rest), jnp.bfloat16)),
        in_specs=[ANY] * 4 + [columns_of(same0), columns_of(relayed0), tile_spec],
        out_specs=(tile_spec, whole(rows, rest)),
        scratch_shapes=[
            pltpu.VMEM((rows, 2 * depth), jnp.bfloat16),
            pltpu.SemaphoreType.DMA((32,)),
        ],
        compiler_params=params(24),
        cost_estimate=matmul_cost(rows, 2 * first, columns, rows * columns * 8),
        name="remote",
    )(remote_x0, remote_x1, remote_y0, remote_y1, same0, relayed0, so_far)

    corrected, power = pl.pallas_call(
        final_kernel,
        grid=grid,
        out_shape=(sums, jax.ShapeDtypeStruct((rows // 128, 128), jnp.float32)),
        in_specs=[ANY] * 2
        + [columns_of(second_factor)] * 2
        + [whole(rows, rest), columns_of(same1), columns_of(relayed1), tile_spec],
        out_specs=(tile_spec, whole(rows // 128, 128)),
        scratch_shapes=eight_slots
        + [pltpu.VMEM((rows, 128), jnp.float32), pltpu.SemaphoreType.DMA((16,))],
        compiler_params=params(60),
        cost_estimate=matmul_cost(rows, 8 * WIDTH + rest, columns, rows * columns * 12),
        name="final",
    )(local_x1, local_y1, second_factor, partner, left_over, same1, relayed1, so_far)

    line = lax.axis_size(("hi", "y", "x"))
    copies = jnp.broadcast_to(power, (line, *power.shape))
    powers = lax.all_to_all(copies, ("hi", "y", "x"), split_axis=0, concat_axis=0, tiled=True)

    scale_spec = pl.BlockSpec((rows, tile), lambda j: (0, j))
    return pl.pallas_call(
        functools.partial(scale_kernel, columns * line),
        grid=(columns // tile,),
        out_shape=jax.ShapeDtypeStruct((rows, columns), jnp.float32),
        in_specs=[pl.BlockSpec(powers.shape, lambda j: (0, 0, 0)), scale_spec],
        out_specs=scale_spec,
        scratch_shapes=[pltpu.VMEM((128, 128), jnp.float32)],
        input_output_aliases={1: 0},
        compiler_params=params(12),
        name="scale",
    )(powers, corrected)


def solution(mesh):
    parts = Mesh(mesh.devices.reshape(2, 2, 2, 4, 4), ("lo", "c", "hi", "y", "x"))
    spec = P(("lo", "c"), ("hi", "y", "x"))

    return jax.shard_map(
        shards, mesh=parts, in_specs=(spec, spec, spec, P()), out_specs=spec, check_vma=False
    )
```

profile of v0, /device:TPU:0, one launch (start us, length us, event | category | flops | bytes accessed | tf_op | source)
XLA Modules:
  0.0 267.0 jit_solution(5366006780348566872)
XLA Ops:
  0.0 3.9 %slice.22 = bf16[1536,1024]{1,0:T(8,128)(2,1)} slice(bf16[2048,1024]{1,0:T(8,128)(2,1)} %mine.3), slice={[0:1536], [0:1024]} | slice | bytes 6291456 | tf_op jit(solution)/shard_map/slice | solution.py:226
  3.9 2.0 collective-permute-start.18
  7.8 3.7 %collective-permute-start.2 = (bf16[1024,256]{1,0:T(8,128)(2,1)S(1)}, bf16[1024,256]{1,0:T(8,128)(2,1)S(1)}, u32[]{:S(2)}, u32[]{:S(2)}) collective-permute-start(bf16[1024,256]{1,0:T(8,128)(2,1)S(1)} %multiply_convert_fusion), channel_id=1, source_target_pairs={{0,16},{16,0},{1,17},{17,1},{2,18},{18,2},{3,19},{19,3},{4,20},{20... | collective-permute-start | bytes 1572872 | tf_op jit(solution)/shard_map/ppermute | solution.py:222
  13.2 75.6 %collective-permute-done.2 = bf16[1024,256]{1,0:T(8,128)(2,1)S(1)} collective-permute-done((bf16[1024,256]{1,0:T(8,128)(2,1)S(1)}, bf16[1024,256]{1,0:T(8,128)(2,1)S(1)}, u32[]{:S(2)}, u32[]{:S(2)}) %collective-permute-start.2) | collective-permute-done | bytes 524320 | tf_op jit(solution)/shard_map/ppermute | solution.py:222
  93.4 2.2 collective-permute-start.8
  96.8 4.2 %collective-permute-start.10 = (bf16[2,512,256]{2,1,0:T(8,128)(2,1)}, bf16[2,512,256]{2,1,0:T(8,128)(2,1)}, u32[]{:S(2)}, u32[]{:S(2)}) collective-permute-start(bf16[2,512,256]{2,1,0:T(8,128)(2,1)} %pad_maximum_fusion.11), channel_id=1, source_target_pairs={{0,12},{4,8},{8,4},{12,0},{32,36},{36,32},{40,44},{44,40},{1,13},{... | collective-permute-start | bytes 1572872 | tf_op jit(solution)/shard_map/ppermute | solution.py:28
  101.7 2.8 %collective-permute-start.3 = (bf16[1,512,256]{2,1,0:T(8,128)(2,1)}, bf16[1,512,256]{2,1,0:T(8,128)(2,1)}, u32[]{:S(2)}, u32[]{:S(2)}) collective-permute-start(bf16[1,512,256]{2,1,0:T(8,128)(2,1)} %get-tuple-element.20), channel_id=1, source_target_pairs={{0,1},{1,0},{2,3},{3,2},{32,35},{33,34},{34,33},{35,32},{4,5},{5,4... | collective-permute-start | bytes 786440 | tf_op jit(solution)/shard_map/ppermute | solution.py:28
  105.6 5.7 %collective-permute-done.3 = bf16[1,512,256]{2,1,0:T(8,128)(2,1)} collective-permute-done((bf16[1,512,256]{2,1,0:T(8,128)(2,1)}, bf16[1,512,256]{2,1,0:T(8,128)(2,1)}, u32[]{:S(2)}, u32[]{:S(2)}) %collective-permute-start.3) | collective-permute-done | bytes 262176 | tf_op jit(solution)/shard_map/ppermute | solution.py:28
  111.3 3.0 %collective-permute-start.1 = (bf16[2,512,256]{2,1,0:T(8,128)(2,1)S(1)}, bf16[2,512,256]{2,1,0:T(8,128)(2,1)S(1)}, u32[]{:S(2)}, u32[]{:S(2)}) collective-permute-start(bf16[2,512,256]{2,1,0:T(8,128)(2,1)S(1)} %pad_maximum_fusion.8), channel_id=1, source_target_pairs={{0,3},{1,2},{2,1},{3,0},{32,33},{33,32},{34,35},{35,34},{4,7},{5,6... | collective-permute-start | bytes 1572872 | tf_op jit(solution)/shard_map/ppermute | solution.py:28
  118.5 8.8 %collective-permute-done.1 = bf16[2,512,256]{2,1,0:T(8,128)(2,1)S(1)} collective-permute-done((bf16[2,512,256]{2,1,0:T(8,128)(2,1)S(1)}, bf16[2,512,256]{2,1,0:T(8,128)(2,1)S(1)}, u32[]{:S(2)}, u32[]{:S(2)}) %collective-permute-start.1) | collective-permute-done | bytes 524320 | tf_op jit(solution)/shard_map/ppermute | solution.py:28
  128.5 10.0 %collective-permute-done.4 = bf16[2,512,256]{2,1,0:T(8,128)(2,1)S(1)} collective-permute-done((bf16[2,512,256]{2,1,0:T(8,128)(2,1)S(1)}, bf16[2,512,256]{2,1,0:T(8,128)(2,1)S(1)}, u32[]{:S(2)}, u32[]{:S(2)}) %collective-permute-start.4) | collective-permute-done | bytes 524320 | tf_op jit(solution)/shard_map/ppermute | solution.py:28
  143.3 13.7 %collective-permute-done.14 = bf16[4,512,256]{2,1,0:T(8,128)(2,1)S(1)} collective-permute-done((bf16[4,512,256]{2,1,0:T(8,128)(2,1)S(1)}, bf16[4,512,256]{2,1,0:T(8,128)(2,1)S(1)}, u32[]{:S(2)}, u32[]{:S(2)}) %collective-permute-start.14) | collective-permute-done | bytes 1048608 | tf_op jit(solution)/shard_map/ppermute | solution.py:28
  157.0 4.2 %collective-permute-start.17 = (bf16[8,512,256]{2,1,0:T(8,128)(2,1)S(1)}, bf16[8,512,256]{2,1,0:T(8,128)(2,1)S(1)}, u32[]{:S(2)}, u32[]{:S(2)}) collective-permute-start(bf16[8,512,256]{2,1,0:T(8,128)(2,1)S(1)} %pad_maximum_fusion.3.y0), channel_id=1, source_target_pairs={{0,3},{1,2},{2,1},{3,0},{32,33},{33,32},{34,35},{35,34},{4,7},{5,6... | collective-permute-start | bytes 6291464 | tf_op jit(solution)/shard_map/ppermute | solution.py:28
  161.3 18.1 %collective-permute-done.5 = bf16[4,512,256]{2,1,0:T(8,128)(2,1)S(1)} collective-permute-done((bf16[4,512,256]{2,1,0:T(8,128)(2,1)S(1)}, bf16[4,512,256]{2,1,0:T(8,128)(2,1)S(1)}, u32[]{:S(2)}, u32[]{:S(2)}) %collective-permute-start.5) | collective-permute-done | bytes 1048608 | tf_op jit(solution)/shard_map/ppermute | solution.py:28
  179.8 4.2 %collective-permute-start.12 = (bf16[8,512,256]{2,1,0:T(8,128)(2,1)S(1)}, bf16[8,512,256]{2,1,0:T(8,128)(2,1)S(1)}, u32[]{:S(2)}, u32[]{:S(2)}) collective-permute-start(bf16[8,512,256]{2,1,0:T(8,128)(2,1)S(1)} %pad_maximum_fusion.1.y0), channel_id=1, source_target_pairs={{0,3},{1,2},{2,1},{3,0},{32,33},{33,32},{34,35},{35,34},{4,7},{5,6... | collective-permute-start | bytes 6291464 | tf_op jit(solution)/shard_map/ppermute | solution.py:28
  184.1 3.2 %collective-permute-start.6 = (bf16[8,512,256]{2,1,0:T(8,128)(2,1)S(1)}, bf16[8,512,256]{2,1,0:T(8,128)(2,1)S(1)}, u32[]{:S(2)}, u32[]{:S(2)}) collective-permute-start(bf16[8,512,256]{2,1,0:T(8,128)(2,1)S(1)} %pad_maximum_fusion.x0), channel_id=1, source_target_pairs={{0,12},{4,8},{8,4},{12,0},{32,36},{36,32},{40,44},{44,40},{1,13},{... | collective-permute-start | bytes 6291464 | tf_op jit(solution)/shard_map/ppermute | solution.py:28
  187.3 8.1 %local.1.so_far = f32[1024,1024]{1,0:T(8,128)S(1)} custom-call(bf16[8,512,256]{2,1,0:T(8,128)(2,1)S(1)} %pad_maximum_fusion.x0, bf16[8,512,256]{2,1,0:T(8,128)(2,1)S(1)} %pad_maximum_fusion.1.y0, bf16[2048,1024]{1,0:T(8,128)(2,1)S(1)} %copy-done, bf16[2048,1024]{1,0:T(8,128)(2,1)} %collective-permute-done.13.partner, f32[1024,1024]{1,0:T(8,128)S(1)} %copy-done.1), custom_call_target="tpu_custom_call" | custom-call | flops 4294967296 | bytes 12582912 | tf_op jit(solution)/shard_map/local/pallas_call | solution.py:261
  195.4 11.3 %collective-permute-done.15.x1 = bf16[8,512,256]{2,1,0:T(8,128)(2,1)S(1)} collective-permute-done((bf16[8,512,256]{2,1,0:T(8,128)(2,1)S(1)}, bf16[8,512,256]{2,1,0:T(8,128)(2,1)S(1)}, u32[]{:S(2)}, u32[]{:S(2)}) %collective-permute-start.15) | collective-permute-done | bytes 2097184 | tf_op jit(solution)/shard_map/ppermute | solution.py:28
  206.7 10.5 %remote.1 = (f32[1024,1024]{1,0:T(8,128)S(1)}, bf16[1024,1024]{1,0:T(8,128)(2,1)S(1)}) custom-call(bf16[8,512,256]{2,1,0:T(8,128)(2,1)S(1)} %pad_maximum_fusion.2.x0, bf16[8,512,256]{2,1,0:T(8,128)(2,1)S(1)} %collective-permute-done.15.x1, bf16[8,512,256]{2,1,0:T(8,128)(2,1)S(1)} %pad_maximum_fusion.3.y0, ...), custom_call_target="tpu_custom_call" | custom-call | flops 6442450944 | bytes 20971520 | tf_op jit(solution)/shard_map/remote/pallas_call | solution.py:274
  217.2 2.0 copy-done.2
  220.6 8.6 %collective-permute-done.6.x1 = bf16[8,512,256]{2,1,0:T(8,128)(2,1)S(1)} collective-permute-done((bf16[8,512,256]{2,1,0:T(8,128)(2,1)S(1)}, bf16[8,512,256]{2,1,0:T(8,128)(2,1)S(1)}, u32[]{:S(2)}, u32[]{:S(2)}) %collective-permute-start.6) | collective-permute-done | bytes 2097184 | tf_op jit(solution)/shard_map/ppermute | solution.py:28
  230.5 15.1 %final.1 = (f32[1024,1024]{1,0:T(8,128)}, f32[8,128]{1,0:T(8,128)}) custom-call(bf16[8,512,256]{2,1,0:T(8,128)(2,1)} %copy-done.15, bf16[8,512,256]{2,1,0:T(8,128)(2,1)} %copy-done.14, bf16[2048,1024]{1,0:T(8,128)(2,1)} %mine.3, bf16[2048,1024]{1,0:T(8,128)(2,1)} %collective-permute-done.13.partner, bf16[1024,1024]{1,0:T(8,128)(2,1)} %copy-done.3, ...), custom_call_target="tpu_custom_call" | custom-call | flops 6442450944 | bytes 25165824 | tf_op jit(solution)/shard_map/final/pallas_call | solution.py:289
  246.3 15.6 %all_to_all.5.power_ref = f32[32,8,128]{2,1,0:T(8,128)S(1)} all-to-all(f32[32,8,128]{2,1,0:T(8,128)S(1)} %broadcast_in_dim.20), channel_id=1, replica_groups=mesh['lo'=2,'c'=2,'hi'=2,'y'=4,'x'=4] {'hi','y','x'}, dimensions={0} | all-to-all | bytes 262144 | tf_op jit(solution)/shard_map/all_to_all | solution.py:306
  261.9 5.0 %scale.1 = f32[1024,1024]{1,0:T(8,128)} custom-call(f32[32,8,128]{2,1,0:T(8,128)S(1)} %all_to_all.5.power_ref, f32[1024,1024]{1,0:T(8,128)} %get-tuple-element.12.corrected_ref), custom_call_target="tpu_custom_call", output_to_operand_aliasing={{}: (1, {})} | custom-call | tf_op jit(solution)/shard_map/scale/pallas_call | solution.py:309
  (76 shorter events, 25.3 us)
Async XLA Ops:
  3.9 138.0 %collective-permute-start.18 = (bf16[1536,1024]{1,0:T(8,128)(2,1)}, bf16[1536,1024]{1,0:T(8,128)(2,1)S(1)}, u32[]{:S(2)}, u32[]{:S(2)}) collective-permute-start(bf16[1536,1024]{1,0:T(8,128)(2,1)} %slice.22), channel_id=1, source_target_pairs={{0,64},{64,0},{1,65},{65,1},{2,66},{66,2},{3,67},{67,3},{4,68},{68... | collective-permute-start | bytes 9437192 | tf_op jit(solution)/shard_map/ppermute | solution.py:226
  7.8 80.9 %collective-permute-start.2 = (bf16[1024,256]{1,0:T(8,128)(2,1)S(1)}, bf16[1024,256]{1,0:T(8,128)(2,1)S(1)}, u32[]{:S(2)}, u32[]{:S(2)}) collective-permute-start(bf16[1024,256]{1,0:T(8,128)(2,1)S(1)} %multiply_convert_fusion), channel_id=1, source_target_pairs={{0,16},{16,0},{1,17},{17,1},{2,18},{18,2},{3,19},{19,3},{4,20},{20... | collective-permute-start | bytes 1572872 | tf_op jit(solution)/shard_map/ppermute | solution.py:222
  11.5 172.6 %collective-permute-start.13 = (bf16[2048,1024]{1,0:T(8,128)(2,1)}, bf16[2048,1024]{1,0:T(8,128)(2,1)}, u32[]{:S(2)}, u32[]{:S(2)}) collective-permute-start(bf16[2048,1024]{1,0:T(8,128)(2,1)} %mine.3), channel_id=1, source_target_pairs={{0,32},{32,0},{1,33},{33,1},{2,34},{34,2},{3,35},{35,3},{4,36},{36... | collective-permute-start | bytes 12582920 | tf_op jit(solution)/shard_map/ppermute | solution.py:228
  11.5 89.5 %copy-start.4 = (bf16[1,512,256]{2,1,0:T(8,128)(2,1)}, bf16[1,512,256]{2,1,0:T(8,128)(2,1)S(1)}, u32[]{:S(2)}) copy-start(bf16[1,512,256]{2,1,0:T(8,128)(2,1)S(1)} %get-tuple-element.17) | copy-start | bytes 786436
  11.5 81.0 %collective-permute-start.7 = (bf16[1,512,256]{2,1,0:T(8,128)(2,1)S(1)}, bf16[1,512,256]{2,1,0:T(8,128)(2,1)S(1)}, u32[]{:S(2)}, u32[]{:S(2)}) collective-permute-start(bf16[1,512,256]{2,1,0:T(8,128)(2,1)S(1)} %get-tuple-element.17), channel_id=1, source_target_pairs={{0,4},{4,0},{8,12},{12,8},{32,44},{36,40},{40,36},{44,32},{1,5},{5... | collective-permute-start | bytes 786440 | tf_op jit(solution)/shard_map/ppermute | solution.py:28
  89.5 6.4 %collective-permute-start.9 = (bf16[1,512,256]{2,1,0:T(8,128)(2,1)S(1)}, bf16[1,512,256]{2,1,0:T(8,128)(2,1)S(1)}, u32[]{:S(2)}, u32[]{:S(2)}) collective-permute-start(bf16[1,512,256]{2,1,0:T(8,128)(2,1)S(1)} %get-tuple-element.19), channel_id=1, source_target_pairs={{0,4},{4,0},{8,12},{12,8},{32,44},{36,40},{40,36},{44,32},{1,5},{5... | collective-permute-start | bytes 786440 | tf_op jit(solution)/shard_map/ppermute | solution.py:28
  91.1 9.9 %collective-permute-start = (bf16[1,512,256]{2,1,0:T(8,128)(2,1)S(1)}, bf16[1,512,256]{2,1,0:T(8,128)(2,1)S(1)}, u32[]{:S(2)}, u32[]{:S(2)}) collective-permute-start(bf16[1,512,256]{2,1,0:T(8,128)(2,1)S(1)} %get-tuple-element.18), channel_id=1, source_target_pairs={{0,1},{1,0},{2,3},{3,2},{32,35},{33,34},{34,33},{35,32},{4,5},{5,4... | collective-permute-start | bytes 786440 | tf_op jit(solution)/shard_map/ppermute | solution.py:28
  93.4 21.9 %collective-permute-start.8 = (bf16[2,512,256]{2,1,0:T(8,128)(2,1)}, bf16[2,512,256]{2,1,0:T(8,128)(2,1)}, u32[]{:S(2)}, u32[]{:S(2)}) collective-permute-start(bf16[2,512,256]{2,1,0:T(8,128)(2,1)} %pad_maximum_fusion.10), channel_id=1, source_target_pairs={{0,12},{4,8},{8,4},{12,0},{32,36},{36,32},{40,44},{44,40},{1,13},{... | collective-permute-start | bytes 1572872 | tf_op jit(solution)/shard_map/ppermute | solution.py:28
  96.8 18.9 %collective-permute-start.10 = (bf16[2,512,256]{2,1,0:T(8,128)(2,1)}, bf16[2,512,256]{2,1,0:T(8,128)(2,1)}, u32[]{:S(2)}, u32[]{:S(2)}) collective-permute-start(bf16[2,512,256]{2,1,0:T(8,128)(2,1)} %pad_maximum_fusion.11), channel_id=1, source_target_pairs={{0,12},{4,8},{8,4},{12,0},{32,36},{36,32},{40,44},{44,40},{1,13},{... | collective-permute-start | bytes 1572872 | tf_op jit(solution)/shard_map/ppermute | solution.py:28
  101.7 9.5 %collective-permute-start.3 = (bf16[1,512,256]{2,1,0:T(8,128)(2,1)}, bf16[1,512,256]{2,1,0:T(8,128)(2,1)}, u32[]{:S(2)}, u32[]{:S(2)}) collective-permute-start(bf16[1,512,256]{2,1,0:T(8,128)(2,1)} %get-tuple-element.20), channel_id=1, source_target_pairs={{0,1},{1,0},{2,3},{3,2},{32,35},{33,34},{34,33},{35,32},{4,5},{5,4... | collective-permute-start | bytes 786440 | tf_op jit(solution)/shard_map/ppermute | solution.py:28
  111.3 16.0 %collective-permute-start.1 = (bf16[2,512,256]{2,1,0:T(8,128)(2,1)S(1)}, bf16[2,512,256]{2,1,0:T(8,128)(2,1)S(1)}, u32[]{:S(2)}, u32[]{:S(2)}) collective-permute-start(bf16[2,512,256]{2,1,0:T(8,128)(2,1)S(1)} %pad_maximum_fusion.8), channel_id=1, source_target_pairs={{0,3},{1,2},{2,1},{3,0},{32,33},{33,32},{34,35},{35,34},{4,7},{5,6... | collective-permute-start | bytes 1572872 | tf_op jit(solution)/shard_map/ppermute | solution.py:28
  115.3 23.2 %copy-start.9 = (bf16[1,512,256]{2,1,0:T(8,128)(2,1)S(1)}, bf16[1,512,256]{2,1,0:T(8,128)(2,1)}, u32[]{:S(2)}) copy-start(bf16[1,512,256]{2,1,0:T(8,128)(2,1)} %copy-done.8) | copy-start | bytes 786436
  115.4 23.2 %collective-permute-start.4 = (bf16[2,512,256]{2,1,0:T(8,128)(2,1)S(1)}, bf16[2,512,256]{2,1,0:T(8,128)(2,1)S(1)}, u32[]{:S(2)}, u32[]{:S(2)}) collective-permute-start(bf16[2,512,256]{2,1,0:T(8,128)(2,1)S(1)} %pad_maximum_fusion.9), channel_id=1, source_target_pairs={{0,3},{1,2},{2,1},{3,0},{32,33},{33,32},{34,35},{35,34},{4,7},{5,6... | collective-permute-start | bytes 1572872 | tf_op jit(solution)/shard_map/ppermute | solution.py:28
  117.1 23.3 %collective-permute-start.16 = (bf16[4,512,256]{2,1,0:T(8,128)(2,1)S(1)}, bf16[4,512,256]{2,1,0:T(8,128)(2,1)S(1)}, u32[]{:S(2)}, u32[]{:S(2)}) collective-permute-start(bf16[4,512,256]{2,1,0:T(8,128)(2,1)S(1)} %get-tuple-element.13), channel_id=1, source_target_pairs={{0,1},{1,0},{2,3},{3,2},{32,35},{33,34},{34,33},{35,32},{4,5},{5,4... | collective-permute-start | bytes 3145736 | tf_op jit(solution)/shard_map/ppermute | solution.py:28
  127.3 16.0 %collective-permute-start.11 = (bf16[4,512,256]{2,1,0:T(8,128)(2,1)S(1)}, bf16[4,512,256]{2,1,0:T(8,128)(2,1)S(1)}, u32[]{:S(2)}, u32[]{:S(2)}) collective-permute-start(bf16[4,512,256]{2,1,0:T(8,128)(2,1)S(1)} %get-tuple-element.14), channel_id=1, source_target_pairs={{0,1},{1,0},{2,3},{3,2},{32,35},{33,34},{34,33},{35,32},{4,5},{5,4... | collective-permute-start | bytes 3145736 | tf_op jit(solution)/shard_map/ppermute | solution.py:28
  139.8 17.2 %collective-permute-start.14 = (bf16[4,512,256]{2,1,0:T(8,128)(2,1)S(1)}, bf16[4,512,256]{2,1,0:T(8,128)(2,1)S(1)}, u32[]{:S(2)}, u32[]{:S(2)}) collective-permute-start(bf16[4,512,256]{2,1,0:T(8,128)(2,1)S(1)} %get-tuple-element.15), channel_id=1, source_target_pairs={{0,4},{4,0},{8,12},{12,8},{32,44},{36,40},{40,36},{44,32},{1,5},{5... | collective-permute-start | bytes 3145736 | tf_op jit(solution)/shard_map/ppermute | solution.py:28
  140.4 39.0 %collective-permute-start.5 = (bf16[4,512,256]{2,1,0:T(8,128)(2,1)S(1)}, bf16[4,512,256]{2,1,0:T(8,128)(2,1)S(1)}, u32[]{:S(2)}, u32[]{:S(2)}) collective-permute-start(bf16[4,512,256]{2,1,0:T(8,128)(2,1)S(1)} %get-tuple-element.16), channel_id=1, source_target_pairs={{0,4},{4,0},{8,12},{12,8},{32,44},{36,40},{40,36},{44,32},{1,5},{5... | collective-permute-start | bytes 3145736 | tf_op jit(solution)/shard_map/ppermute | solution.py:28
  141.9 64.8 %collective-permute-start.19 = (bf16[1536,1024]{1,0:T(8,128)(2,1)S(1)}, bf16[1536,1024]{1,0:T(8,128)(2,1)S(1)}, u32[]{:S(2)}, u32[]{:S(2)}) collective-permute-start(bf16[1536,1024]{1,0:T(8,128)(2,1)S(1)} %collective-permute-done.18.same), channel_id=1, source_target_pairs={{0,32},{32,0},{1,33},{33,1},{2,34},{34,2},{3,35},{35,3},{4,36},{36... | collective-permute-start | bytes 9437192 | tf_op jit(solution)/shard_map/ppermute | solution.py:229
  143.3 36.6 %collective-permute-start.20 = (bf16[512,1024]{1,0:T(8,128)(2,1)S(1)}, bf16[512,1024]{1,0:T(8,128)(2,1)}, u32[]{:S(2)}, u32[]{:S(2)}) collective-permute-start(bf16[512,1024]{1,0:T(8,128)(2,1)S(1)} %slice.23), channel_id=1, source_target_pairs={{0,64},{64,0},{1,65},{65,1},{2,66},{66,2},{3,67},{67,3},{4,68},{68... | collective-permute-start | bytes 3145736 | tf_op jit(solution)/shard_map/ppermute | solution.py:227
  157.0 30.4 %collective-permute-start.17 = (bf16[8,512,256]{2,1,0:T(8,128)(2,1)S(1)}, bf16[8,512,256]{2,1,0:T(8,128)(2,1)S(1)}, u32[]{:S(2)}, u32[]{:S(2)}) collective-permute-start(bf16[8,512,256]{2,1,0:T(8,128)(2,1)S(1)} %pad_maximum_fusion.3.y0), channel_id=1, source_target_pairs={{0,3},{1,2},{2,1},{3,0},{32,33},{33,32},{34,35},{35,34},{4,7},{5,6... | collective-permute-start | bytes 6291464 | tf_op jit(solution)/shard_map/ppermute | solution.py:28
  179.4 27.2 %collective-permute-start.15 = (bf16[8,512,256]{2,1,0:T(8,128)(2,1)S(1)}, bf16[8,512,256]{2,1,0:T(8,128)(2,1)S(1)}, u32[]{:S(2)}, u32[]{:S(2)}) collective-permute-start(bf16[8,512,256]{2,1,0:T(8,128)(2,1)S(1)} %pad_maximum_fusion.2.x0), channel_id=1, source_target_pairs={{0,12},{4,8},{8,4},{12,0},{32,36},{36,32},{40,44},{44,40},{1,13},{... | collective-permute-start | bytes 6291464 | tf_op jit(solution)/shard_map/ppermute | solution.py:28
  179.8 40.7 %collective-permute-start.12 = (bf16[8,512,256]{2,1,0:T(8,128)(2,1)S(1)}, bf16[8,512,256]{2,1,0:T(8,128)(2,1)S(1)}, u32[]{:S(2)}, u32[]{:S(2)}) collective-permute-start(bf16[8,512,256]{2,1,0:T(8,128)(2,1)S(1)} %pad_maximum_fusion.1.y0), channel_id=1, source_target_pairs={{0,3},{1,2},{2,1},{3,0},{32,33},{33,32},{34,35},{35,34},{4,7},{5,6... | collective-permute-start | bytes 6291464 | tf_op jit(solution)/shard_map/ppermute | solution.py:28
  184.1 45.1 %collective-permute-start.6 = (bf16[8,512,256]{2,1,0:T(8,128)(2,1)S(1)}, bf16[8,512,256]{2,1,0:T(8,128)(2,1)S(1)}, u32[]{:S(2)}, u32[]{:S(2)}) collective-permute-start(bf16[8,512,256]{2,1,0:T(8,128)(2,1)S(1)} %pad_maximum_fusion.x0), channel_id=1, source_target_pairs={{0,12},{4,8},{8,4},{12,0},{32,36},{36,32},{40,44},{44,40},{1,13},{... | collective-permute-start | bytes 6291464 | tf_op jit(solution)/shard_map/ppermute | solution.py:28
  187.3 33.2 %collective-permute-start.21 = (bf16[512,1024]{1,0:T(8,128)(2,1)}, bf16[512,1024]{1,0:T(8,128)(2,1)S(1)}, u32[]{:S(2)}, u32[]{:S(2)}) collective-permute-start(bf16[512,1024]{1,0:T(8,128)(2,1)} %collective-permute-done.20.same), channel_id=1, source_target_pairs={{0,32},{32,0},{1,33},{33,1},{2,34},{34,2},{3,35},{35,3},{4,36},{36... | collective-permute-start | bytes 3145736 | tf_op jit(solution)/shard_map/ppermute | solution.py:230
  (15 other events, 114.9 us)
where the time goes:
time: 267 us
  waiting for transfers between devices  153 us (57%)
  starting transfers between devices  39.3 us (15%)
  Pallas kernels  38.8 us (15%)
  blocking collectives  15.6 us (6%)
  local copies, waits for them, and re-layouts  11.6 us (4%)
  other arithmetic  8.5 us (3%)
    ppermute x16, waiting for transfers between devices, exchange(): return lax.ppermute(block, ('c', axis), pairs)  77.5 us
    ppermute x1, waiting for transfers between devices, shards(): foreign = lax.ppermute(scaled, 'hi', [(0, 1), (1, 0)])  75.6 us
    ppermute x16, starting transfers between devices, exchange(): return lax.ppermute(block, ('c', axis), pairs)  33.6 us
    all_to_all x1, blocking collectives, shards(): lax.all_to_all(copies, ('hi', 'y', 'x'), split_axis=0, concat_axis=0, til...  15.6 us
    pallas_call x1, Pallas kernels, shards(): pl.pallas_call(final_kernel, grid=grid, out_shape=(sums, jax.ShapeDtypeSt...  15.1 us
    pallas_call x1, Pallas kernels, shards(): pl.pallas_call(remote_kernel, grid=grid, out_shape=(sums, jax.ShapeDtypeS...  10.5 us
    pallas_call x1, Pallas kernels, shards(): pl.pallas_call(local_kernel, grid=grid, out_shape=sums, in_specs=[ANY] *...  8.07 us
    unnamed x34, local copies, waits for them, and re-layouts  5.4 us
  transfers between devices with their start and end apart: 22, of which 10 were waited for; matrix products, arithmetic and copies ran while one was open for 4% of the time, Pallas kernels for 7%

commit v1 on v0

--- a/solution.py
+++ b/solution.py
@@ -81,54 +81,24 @@
     return copies
 
 
-def load_slots(parts, left, sems):
-    rows = left.shape[0] // 2
-    return [
-        pltpu.make_async_copy(
-            parts[colour].at[slot],
-            left.at[pl.ds(colour * rows, rows), pl.ds(slot * WIDTH, WIDTH)],
-            sems.at[colour * 8 + slot],
-        )
-        for colour in range(2)
-        for slot in range(8)
-    ]
-
-
 def product(left, right):
     return jnp.dot(left, right, preferred_element_type=jnp.float32)
 
 
-def slot_product(left, mine, partner, colour, first_slot):
-    rows = left.shape[0] // 2
-    depth = mine.shape[0]
+def slot_product(left, local, colour, first_slot):
     total = None
     for slot in range(8):
-        begin = slot_columns(first_slot + slot, colour == 0)
-        here = pl.multiple_of(jnp.minimum(begin, depth - WIDTH), WIDTH)
-        there = pl.multiple_of(jnp.maximum(begin - depth, 0), WIDTH)
-        right = jnp.where(
-            begin < depth, mine[pl.ds(here, WIDTH), :], partner[pl.ds(there, WIDTH), :]
-        )
-        term = product(
-            left[colour * rows : (colour + 1) * rows, slot * WIDTH : (slot + 1) * WIDTH], right
-        )
+        begin = pl.multiple_of(slot_columns(first_slot + slot, colour == 0), WIDTH)
+        term = product(left[slot], local[pl.ds(begin, WIDTH), :])
         total = term if total is None else total + term
     return total
 
 
-def local_kernel(x0, y0, mine, partner, result_ref, out_ref, left, sems):
-    @pl.when(pl.program_id(0) == 0)
-    def _():
-        copies = load_slots((x0, y0), left, sems)
-        for copy in copies:
-            copy.start()
-        for copy in copies:
-            copy.wait()
-
-    rows = left.shape[0] // 2
-    for colour in range(2):
+def local_kernel(x0, y0, local, result_ref, out_ref):
+    rows = x0.shape[1]
+    for colour, left in enumerate((x0, y0)):
         here = slice(colour * rows, (colour + 1) * rows)
-        out_ref[here, :] = result_ref[here, :] - slot_product(left, mine, partner, colour, 0)
+        out_ref[here, :] = result_ref[here, :] - slot_product(left, local, colour, 0)
 
 
 def remote_kernel(x0, x1, y0, y1, same, relayed, so_far, out_ref, rest_ref, left, sems):
@@ -151,26 +121,19 @@
     )
 
 
-def final_kernel(
-    x1, y1, mine, partner, rest, same, relayed, so_far, out_ref, power_ref, left, power, sems
-):
+def final_kernel(x1, y1, local, rest, same, relayed, so_far, out_ref, power_ref, power):
     step = pl.program_id(0)
     last = same.shape[0]
 
     @pl.when(step == 0)
     def _():
-        copies = load_slots((x1, y1), left, sems)
-        for copy in copies:
-            copy.start()
         power[...] = jnp.zeros_like(power)
-        for copy in copies:
-            copy.wait()
-
-    rows = left.shape[0] // 2
+
+    rows = x1.shape[1]
     lanes = power.shape[1]
-    for colour in range(2):
+    for colour, left in enumerate((x1, y1)):
         here = slice(colour * rows, (colour + 1) * rows)
-        total = slot_product(left, mine, partner, colour, 8)
+        total = slot_product(left, local, colour, 8)
         total += product(rest[here, :last], same[...]) + product(rest[here, last:], relayed[...])
         corrected = so_far[here, :] - total
         out_ref[here, :] = corrected
@@ -229,6 +192,8 @@
     relayed0 = lax.ppermute(same0, "c", swap)
     relayed1 = lax.ppermute(same1, "c", swap)
 
+    local = jnp.concatenate([second_factor, partner])
+
     def lines(block):
         return (spread_line(block[None, :half], "x"), spread_line(block[None, half:], "y"))
 
@@ -252,23 +217,24 @@
         return pl.BlockSpec((array.shape[0], tile), lambda j: (0, j))
 
     def whole(*shape):
-        return pl.BlockSpec(shape, lambda j: (0,) * len(shape))
+        return pl.BlockSpec(
+            shape, lambda j: (0,) * len(shape), pipeline_mode=pl.Buffered(1)
+        )
 
     grid = (columns // tile,)
     sums = jax.ShapeDtypeStruct((rows, columns), jnp.float32)
     tile_spec = columns_of(sums)
-    eight_slots = [pltpu.VMEM((rows, 8 * WIDTH), jnp.bfloat16)]
+    slots = whole(8, half, WIDTH)
     so_far = pl.pallas_call(
         local_kernel,
         grid=grid,
         out_shape=sums,
-        in_specs=[ANY] * 2 + [columns_of(second_factor)] * 2 + [tile_spec],
+        in_specs=[slots] * 2 + [columns_of(local), tile_spec],
         out_specs=tile_spec,
-        scratch_shapes=eight_slots + [pltpu.SemaphoreType.DMA((16,))],
-        compiler_params=params(16),
+        compiler_params=params(22),
         cost_estimate=matmul_cost(rows, 8 * WIDTH, columns, rows * columns * 4),
         name="local",
-    )(local_x0, local_y0, second_factor, partner, result_in)
+    )(local_x0, local_y0, local, result_in)
 
     rest = 2 * (depth - first)
     so_far, left_over = pl.pallas_call(
@@ -276,13 +242,14 @@
         grid=grid,
         out_shape=(sums, jax.ShapeDtypeStruct((rows, rest), jnp.bfloat16)),
         in_specs=[ANY] * 4 + [columns_of(same0), columns_of(relayed0), tile_spec],
-        out_specs=(tile_spec, whole(rows, rest)),
+        out_specs=(tile_spec, pl.BlockSpec((rows, rest), lambda j: (0, 0))),
         scratch_shapes=[
             pltpu.VMEM((rows, 2 * depth), jnp.bfloat16),
             pltpu.SemaphoreType.DMA((32,)),
         ],
-        compiler_params=params(24),
+        compiler_params=params(22),
         cost_estimate=matmul_cost(rows, 2 * first, columns, rows * columns * 8),
+        input_output_aliases={6: 0},
         name="remote",
     )(remote_x0, remote_x1, remote_y0, remote_y1, same0, relayed0, so_far)
 
@@ -290,16 +257,16 @@
         final_kernel,
         grid=grid,
         out_shape=(sums, jax.ShapeDtypeStruct((rows // 128, 128), jnp.float32)),
-        in_specs=[ANY] * 2
-        + [columns_of(second_factor)] * 2
-        + [whole(rows, rest), columns_of(same1), columns_of(relayed1), tile_spec],
-        out_specs=(tile_spec, whole(rows // 128, 128)),
-        scratch_shapes=eight_slots
-        + [pltpu.VMEM((rows, 128), jnp.float32), pltpu.SemaphoreType.DMA((16,))],
-        compiler_params=params(60),
+        in_specs=[slots] * 2
+        + [columns_of(local), whole(rows, rest), columns_of(same1), columns_of(relayed1)]
+        + [tile_spec],
+        out_specs=(tile_spec, pl.BlockSpec((rows // 128, 128), lambda j: (0, 0))),
+        scratch_shapes=[pltpu.VMEM((rows, 128), jnp.float32)],
+        compiler_params=params(22),
         cost_estimate=matmul_cost(rows, 8 * WIDTH + rest, columns, rows * columns * 12),
+        input_output_aliases={6: 0},
         name="final",
-    )(local_x1, local_y1, second_factor, partner, left_over, same1, relayed1, so_far)
+    )(local_x1, local_y1, local, left_over, same1, relayed1, so_far)
 
     line = lax.axis_size(("hi", "y", "x"))
     copies = jnp.broadcast_to(power, (line, *power.shape))
@@ -313,8 +280,7 @@
         in_specs=[pl.BlockSpec(powers.shape, lambda j: (0, 0, 0)), scale_spec],
         out_specs=scale_spec,
         scratch_shapes=[pltpu.VMEM((128, 128), jnp.float32)],
-        input_output_aliases={1: 0},
-        compiler_params=params(12),
+        compiler_params=params(22),
         name="scale",
     )(powers, corrected)
 

time: 267 us -> 257 us (0.963)
  Pallas kernels: 38.8 us -> 32.8 us
  waiting for transfers between devices: 153 us -> 148 us
    ppermute x16, waiting for transfers between devices: 77.5 us -> 72.3 us  [exchange(): return lax.ppermute(block, ('c', axis), pairs)]
    pallas_call x1, Pallas kernels: 15.1 us -> 11.4 us  [shards(): pl.pallas_call(final_kernel, grid=grid, out_shape=(sums, jax.ShapeDtypeSt...]
    concatenate x0 -> x1, local copies, waits for them, and re-layouts: none -> 3.29 us  [shards(): local = jnp.concatenate([second_factor, partner])]
    unnamed x34 -> x33, local copies, waits for them, and re-layouts: 5.4 us -> 6.06 us
  transfers between devices with their start and end apart: 22 -> 22, of which waited for: 10 -> 10; matrix products, arithmetic and copies ran while one was open for 4% -> 5% of each run, Pallas kernels for 7% -> 7%
where the time goes in v1:
time: 257 us
  waiting for transfers between devices  148 us (58%)
  starting transfers between devices  38.7 us (15%)
  Pallas kernels  32.8 us (13%)
  blocking collectives  16 us (6%)
  local copies, waits for them, and re-layouts  13.2 us (5%)
  other arithmetic  8.52 us (3%)
    ppermute x1, waiting for transfers between devices, shards(): foreign = lax.ppermute(scaled, 'hi', [(0, 1), (1, 0)])  75.4 us
    ppermute x16, waiting for transfers between devices, exchange(): return lax.ppermute(block, ('c', axis), pairs)  72.3 us
    ppermute x16, starting transfers between devices, exchange(): return lax.ppermute(block, ('c', axis), pairs)  32.9 us
    all_to_all x1, blocking collectives, shards(): lax.all_to_all(copies, ('hi', 'y', 'x'), split_axis=0, concat_axis=0, til...  16 us
    pallas_call x1, Pallas kernels, shards(): pl.pallas_call(final_kernel, grid=grid, out_shape=(sums, jax.ShapeDtypeSt...  11.4 us
    pallas_call x1, Pallas kernels, shards(): pl.pallas_call(remote_kernel, grid=grid, out_shape=(sums, jax.ShapeDtypeS...  11.4 us
    pallas_call x1, Pallas kernels, shards(): pl.pallas_call(local_kernel, grid=grid, out_shape=sums, in_specs=[slots]...  6.99 us
    unnamed x33, local copies, waits for them, and re-layouts  6.06 us
  transfers between devices with their start and end apart: 22, of which 10 were waited for; matrix products, arithmetic and copies ran while one was open for 5% of the time, Pallas kernels for 7%

profile of v1, /device:TPU:0, one launch (start us, length us, event | category | flops | bytes accessed | tf_op | source)
XLA Modules:
  0.0 257.1 jit_solution(1796737767873415908)
XLA Ops:
  0.0 2.2 slice.22
  2.2 2.1 collective-permute-start.18
  6.2 3.7 %collective-permute-start.2 = (bf16[1024,256]{1,0:T(8,128)(2,1)S(1)}, bf16[1024,256]{1,0:T(8,128)(2,1)S(1)}, u32[]{:S(2)}, u32[]{:S(2)}) collective-permute-start(bf16[1024,256]{1,0:T(8,128)(2,1)S(1)} %multiply_convert_fusion), channel_id=1, source_target_pairs={{0,16},{16,0},{1,17},{17,1},{2,18},{18,2},{3,19},{19,3},{4,20},{20... | collective-permute-start | bytes 1572872 | tf_op jit(solution)/shard_map/ppermute | solution.py:185
  11.6 75.4 %collective-permute-done.2 = bf16[1024,256]{1,0:T(8,128)(2,1)S(1)} collective-permute-done((bf16[1024,256]{1,0:T(8,128)(2,1)S(1)}, bf16[1024,256]{1,0:T(8,128)(2,1)S(1)}, u32[]{:S(2)}, u32[]{:S(2)}) %collective-permute-start.2) | collective-permute-done | bytes 524320 | tf_op jit(solution)/shard_map/ppermute | solution.py:185
  91.7 2.2 collective-permute-start.8
  94.9 4.2 %collective-permute-start.10 = (bf16[2,512,256]{2,1,0:T(8,128)(2,1)}, bf16[2,512,256]{2,1,0:T(8,128)(2,1)}, u32[]{:S(2)}, u32[]{:S(2)}) collective-permute-start(bf16[2,512,256]{2,1,0:T(8,128)(2,1)} %pad_maximum_fusion.11), channel_id=1, source_target_pairs={{0,12},{4,8},{8,4},{12,0},{32,36},{36,32},{40,44},{44,40},{1,13},{... | collective-permute-start | bytes 1572872 | tf_op jit(solution)/shard_map/ppermute | solution.py:28
  99.8 2.8 %collective-permute-start.3 = (bf16[1,512,256]{2,1,0:T(8,128)(2,1)}, bf16[1,512,256]{2,1,0:T(8,128)(2,1)}, u32[]{:S(2)}, u32[]{:S(2)}) collective-permute-start(bf16[1,512,256]{2,1,0:T(8,128)(2,1)} %get-tuple-element.20), channel_id=1, source_target_pairs={{0,1},{1,0},{2,3},{3,2},{32,35},{33,34},{34,33},{35,32},{4,5},{5,4... | collective-permute-start | bytes 786440 | tf_op jit(solution)/shard_map/ppermute | solution.py:28
  103.7 5.6 %collective-permute-done.3 = bf16[1,512,256]{2,1,0:T(8,128)(2,1)} collective-permute-done((bf16[1,512,256]{2,1,0:T(8,128)(2,1)}, bf16[1,512,256]{2,1,0:T(8,128)(2,1)}, u32[]{:S(2)}, u32[]{:S(2)}) %collective-permute-start.3) | collective-permute-done | bytes 262176 | tf_op jit(solution)/shard_map/ppermute | solution.py:28
  109.3 3.1 %collective-permute-start.1 = (bf16[2,512,256]{2,1,0:T(8,128)(2,1)S(1)}, bf16[2,512,256]{2,1,0:T(8,128)(2,1)S(1)}, u32[]{:S(2)}, u32[]{:S(2)}) collective-permute-start(bf16[2,512,256]{2,1,0:T(8,128)(2,1)S(1)} %pad_maximum_fusion.8), channel_id=1, source_target_pairs={{0,3},{1,2},{2,1},{3,0},{32,33},{33,32},{34,35},{35,34},{4,7},{5,6... | collective-permute-start | bytes 1572872 | tf_op jit(solution)/shard_map/ppermute | solution.py:28
  116.5 8.8 %collective-permute-done.1 = bf16[2,512,256]{2,1,0:T(8,128)(2,1)S(1)} collective-permute-done((bf16[2,512,256]{2,1,0:T(8,128)(2,1)S(1)}, bf16[2,512,256]{2,1,0:T(8,128)(2,1)S(1)}, u32[]{:S(2)}, u32[]{:S(2)}) %collective-permute-start.1) | collective-permute-done | bytes 524320 | tf_op jit(solution)/shard_map/ppermute | solution.py:28
  126.6 10.0 %collective-permute-done.4 = bf16[2,512,256]{2,1,0:T(8,128)(2,1)S(1)} collective-permute-done((bf16[2,512,256]{2,1,0:T(8,128)(2,1)S(1)}, bf16[2,512,256]{2,1,0:T(8,128)(2,1)S(1)}, u32[]{:S(2)}, u32[]{:S(2)}) %collective-permute-start.4) | collective-permute-done | bytes 524320 | tf_op jit(solution)/shard_map/ppermute | solution.py:28
  141.3 3.2 %collective-permute-start.17 = (bf16[8,512,256]{2,1,0:T(8,128)(2,1)S(1)}, bf16[8,512,256]{2,1,0:T(8,128)(2,1)S(1)}, u32[]{:S(2)}, u32[]{:S(2)}) collective-permute-start(bf16[8,512,256]{2,1,0:T(8,128)(2,1)S(1)} %pad_maximum_fusion.3.y0), channel_id=1, source_target_pairs={{0,3},{1,2},{2,1},{3,0},{32,33},{33,32},{34,35},{35,34},{4,7},{5,6... | collective-permute-start | bytes 6291464 | tf_op jit(solution)/shard_map/ppermute | solution.py:28
  144.6 9.8 %collective-permute-done.14 = bf16[4,512,256]{2,1,0:T(8,128)(2,1)S(1)} collective-permute-done((bf16[4,512,256]{2,1,0:T(8,128)(2,1)S(1)}, bf16[4,512,256]{2,1,0:T(8,128)(2,1)S(1)}, u32[]{:S(2)}, u32[]{:S(2)}) %collective-permute-start.14) | collective-permute-done | bytes 1048608 | tf_op jit(solution)/shard_map/ppermute | solution.py:28
  154.5 22.3 %collective-permute-done.5 = bf16[4,512,256]{2,1,0:T(8,128)(2,1)S(1)} collective-permute-done((bf16[4,512,256]{2,1,0:T(8,128)(2,1)S(1)}, bf16[4,512,256]{2,1,0:T(8,128)(2,1)S(1)}, u32[]{:S(2)}, u32[]{:S(2)}) %collective-permute-start.5) | collective-permute-done | bytes 1048608 | tf_op jit(solution)/shard_map/ppermute | solution.py:28
  177.2 4.6 %collective-permute-start.12 = (bf16[8,512,256]{2,1,0:T(8,128)(2,1)S(1)}, bf16[8,512,256]{2,1,0:T(8,128)(2,1)}, u32[]{:S(2)}, u32[]{:S(2)}) collective-permute-start(bf16[8,512,256]{2,1,0:T(8,128)(2,1)S(1)} %pad_maximum_fusion.1.y0), channel_id=1, source_target_pairs={{0,3},{1,2},{2,1},{3,0},{32,33},{33,32},{34,35},{35,34},{4,7},{5,6... | collective-permute-start | bytes 6291464 | tf_op jit(solution)/shard_map/ppermute | solution.py:28
  181.8 3.2 %collective-permute-start.6 = (bf16[8,512,256]{2,1,0:T(8,128)(2,1)S(1)}, bf16[8,512,256]{2,1,0:T(8,128)(2,1)}, u32[]{:S(2)}, u32[]{:S(2)}) collective-permute-start(bf16[8,512,256]{2,1,0:T(8,128)(2,1)S(1)} %pad_maximum_fusion.x0), channel_id=1, source_target_pairs={{0,12},{4,8},{8,4},{12,0},{32,36},{36,32},{40,44},{44,40},{1,13},{... | collective-permute-start | bytes 6291464 | tf_op jit(solution)/shard_map/ppermute | solution.py:28
  186.9 3.3 %constant_dynamic-update-slice_fusion.local = bf16[4096,1024]{1,0:T(8,128)(2,1)S(1)} fusion(bf16[4096,1024]{1,0:T(8,128)(2,1)S(1)} %constant_dynamic-update-slice_fusion.1, bf16[2048,1024]{1,0:T(8,128)(2,1)} %collective-permute-done.13), kind=kLoop, calls=%fused_computation.21 | loop fusion | bytes 8388608 | tf_op jit(solution)/shard_map/concatenate | solution.py:195
  190.2 7.0 %local.1.so_far = f32[1024,1024]{1,0:T(8,128)S(1)} custom-call(bf16[8,512,256]{2,1,0:T(8,128)(2,1)S(1)} %pad_maximum_fusion.x0, bf16[8,512,256]{2,1,0:T(8,128)(2,1)S(1)} %pad_maximum_fusion.1.y0, bf16[4096,1024]{1,0:T(8,128)(2,1)S(1)} %constant_dynamic-update-slice_fusion.local, f32[1024,1024]{1,0:T(8,128)S(1)} %copy-done), custom_call_target="tpu_custom_call" | custom-call | flops 4294967296 | bytes 12582912 | tf_op jit(solution)/shard_map/local/pallas_call | solution.py:228
  197.2 7.0 %collective-permute-done.15.x1 = bf16[8,512,256]{2,1,0:T(8,128)(2,1)} collective-permute-done((bf16[8,512,256]{2,1,0:T(8,128)(2,1)S(1)}, bf16[8,512,256]{2,1,0:T(8,128)(2,1)}, u32[]{:S(2)}, u32[]{:S(2)}) %collective-permute-start.15) | collective-permute-done | bytes 2097184 | tf_op jit(solution)/shard_map/ppermute | solution.py:28
  207.7 11.4 %remote.1 = (f32[1024,1024]{1,0:T(8,128)S(1)}, bf16[1024,1024]{1,0:T(8,128)(2,1)S(1)}) custom-call(bf16[8,512,256]{2,1,0:T(8,128)(2,1)S(1)} %pad_maximum_fusion.2.x0, bf16[8,512,256]{2,1,0:T(8,128)(2,1)} %collective-permute-done.15.x1, bf16[8,512,256]{2,1,0:T(8,128)(2,1)S(1)} %pad_maximum_fusion.3.y0, ...), custom_call_target="tpu_custom_call", output_to_operand_aliasing={{0}: (6, {})} | custom-call | flops 6442450944 | bytes 20971520 | tf_op jit(solution)/shard_map/remote/pallas_call | solution.py:240
  219.1 7.5 %collective-permute-done.6.x1 = bf16[8,512,256]{2,1,0:T(8,128)(2,1)} collective-permute-done((bf16[8,512,256]{2,1,0:T(8,128)(2,1)S(1)}, bf16[8,512,256]{2,1,0:T(8,128)(2,1)}, u32[]{:S(2)}, u32[]{:S(2)}) %collective-permute-start.6) | collective-permute-done | bytes 2097184 | tf_op jit(solution)/shard_map/ppermute | solution.py:28
  226.6 11.4 %final.1 = (f32[1024,1024]{1,0:T(8,128)S(1)}, f32[8,128]{1,0:T(8,128)S(1)}) custom-call(bf16[8,512,256]{2,1,0:T(8,128)(2,1)} %collective-permute-done.6.x1, bf16[8,512,256]{2,1,0:T(8,128)(2,1)} %collective-permute-done.12.y1, bf16[4096,1024]{1,0:T(8,128)(2,1)S(1)} %constant_dynamic-update-slice_fusion.local, ...), custom_call_target="tpu_custom_call", output_to_operand_aliasing={{0}: (6, {})} | custom-call | flops 6442450944 | bytes 25165824 | tf_op jit(solution)/shard_map/final/pallas_call | solution.py:256
  238.1 16.0 %all_to_all.5.power_ref = f32[32,8,128]{2,1,0:T(8,128)S(1)} all-to-all(f32[32,8,128]{2,1,0:T(8,128)S(1)} %broadcast_in_dim.20), channel_id=1, replica_groups=mesh['lo'=2,'c'=2,'hi'=2,'y'=4,'x'=4] {'hi','y','x'}, dimensions={0} | all-to-all | bytes 262144 | tf_op jit(solution)/shard_map/all_to_all | solution.py:273
  254.0 3.0 %scale.1 = f32[1024,1024]{1,0:T(8,128)} custom-call(f32[32,8,128]{2,1,0:T(8,128)S(1)} %all_to_all.5.power_ref, f32[1024,1024]{1,0:T(8,128)S(1)} %get-tuple-element.12.corrected_ref), custom_call_target="tpu_custom_call" | custom-call | tf_op jit(solution)/shard_map/scale/pallas_call | solution.py:276
  (76 shorter events, 27.3 us)
Async XLA Ops:
  2.2 137.7 %collective-permute-start.18 = (bf16[1536,1024]{1,0:T(8,128)(2,1)S(1)}, bf16[1536,1024]{1,0:T(8,128)(2,1)}, u32[]{:S(2)}, u32[]{:S(2)}) collective-permute-start(bf16[1536,1024]{1,0:T(8,128)(2,1)S(1)} %slice.22), channel_id=1, source_target_pairs={{0,64},{64,0},{1,65},{65,1},{2,66},{66,2},{3,67},{67,3},{4,68},{68... | collective-permute-start | bytes 9437192 | tf_op jit(solution)/shard_map/ppermute | solution.py:189
  6.2 80.7 %collective-permute-start.2 = (bf16[1024,256]{1,0:T(8,128)(2,1)S(1)}, bf16[1024,256]{1,0:T(8,128)(2,1)S(1)}, u32[]{:S(2)}, u32[]{:S(2)}) collective-permute-start(bf16[1024,256]{1,0:T(8,128)(2,1)S(1)} %multiply_convert_fusion), channel_id=1, source_target_pairs={{0,16},{16,0},{1,17},{17,1},{2,18},{18,2},{3,19},{19,3},{4,20},{20... | collective-permute-start | bytes 1572872 | tf_op jit(solution)/shard_map/ppermute | solution.py:185
  9.9 171.9 %collective-permute-start.13 = (bf16[2048,1024]{1,0:T(8,128)(2,1)}, bf16[2048,1024]{1,0:T(8,128)(2,1)}, u32[]{:S(2)}, u32[]{:S(2)}) collective-permute-start(bf16[2048,1024]{1,0:T(8,128)(2,1)} %param.5), channel_id=1, source_target_pairs={{0,32},{32,0},{1,33},{33,1},{2,34},{34,2},{3,35},{35,3},{4,36},{36... | collective-permute-start | bytes 12582920 | tf_op jit(solution)/shard_map/ppermute | solution.py:191
  9.9 89.2 %copy-start.6 = (bf16[1,512,256]{2,1,0:T(8,128)(2,1)}, bf16[1,512,256]{2,1,0:T(8,128)(2,1)S(1)}, u32[]{:S(2)}) copy-start(bf16[1,512,256]{2,1,0:T(8,128)(2,1)S(1)} %get-tuple-element.17) | copy-start | bytes 786436
  9.9 80.8 %collective-permute-start.7 = (bf16[1,512,256]{2,1,0:T(8,128)(2,1)S(1)}, bf16[1,512,256]{2,1,0:T(8,128)(2,1)S(1)}, u32[]{:S(2)}, u32[]{:S(2)}) collective-permute-start(bf16[1,512,256]{2,1,0:T(8,128)(2,1)S(1)} %get-tuple-element.17), channel_id=1, source_target_pairs={{0,4},{4,0},{8,12},{12,8},{32,44},{36,40},{40,36},{44,32},{1,5},{5... | collective-permute-start | bytes 786440 | tf_op jit(solution)/shard_map/ppermute | solution.py:28
  87.7 6.4 %collective-permute-start.9 = (bf16[1,512,256]{2,1,0:T(8,128)(2,1)S(1)}, bf16[1,512,256]{2,1,0:T(8,128)(2,1)S(1)}, u32[]{:S(2)}, u32[]{:S(2)}) collective-permute-start(bf16[1,512,256]{2,1,0:T(8,128)(2,1)S(1)} %get-tuple-element.19), channel_id=1, source_target_pairs={{0,4},{4,0},{8,12},{12,8},{32,44},{36,40},{40,36},{44,32},{1,5},{5... | collective-permute-start | bytes 786440 | tf_op jit(solution)/shard_map/ppermute | solution.py:28
  89.3 9.9 %collective-permute-start = (bf16[1,512,256]{2,1,0:T(8,128)(2,1)S(1)}, bf16[1,512,256]{2,1,0:T(8,128)(2,1)S(1)}, u32[]{:S(2)}, u32[]{:S(2)}) collective-permute-start(bf16[1,512,256]{2,1,0:T(8,128)(2,1)S(1)} %get-tuple-element.18), channel_id=1, source_target_pairs={{0,1},{1,0},{2,3},{3,2},{32,35},{33,34},{34,33},{35,32},{4,5},{5,4... | collective-permute-start | bytes 786440 | tf_op jit(solution)/shard_map/ppermute | solution.py:28
  91.7 21.8 %collective-permute-start.8 = (bf16[2,512,256]{2,1,0:T(8,128)(2,1)}, bf16[2,512,256]{2,1,0:T(8,128)(2,1)}, u32[]{:S(2)}, u32[]{:S(2)}) collective-permute-start(bf16[2,512,256]{2,1,0:T(8,128)(2,1)} %pad_maximum_fusion.10), channel_id=1, source_target_pairs={{0,12},{4,8},{8,4},{12,0},{32,36},{36,32},{40,44},{44,40},{1,13},{... | collective-permute-start | bytes 1572872 | tf_op jit(solution)/shard_map/ppermute | solution.py:28
  94.9 18.8 %collective-permute-start.10 = (bf16[2,512,256]{2,1,0:T(8,128)(2,1)}, bf16[2,512,256]{2,1,0:T(8,128)(2,1)}, u32[]{:S(2)}, u32[]{:S(2)}) collective-permute-start(bf16[2,512,256]{2,1,0:T(8,128)(2,1)} %pad_maximum_fusion.11), channel_id=1, source_target_pairs={{0,12},{4,8},{8,4},{12,0},{32,36},{36,32},{40,44},{44,40},{1,13},{... | collective-permute-start | bytes 1572872 | tf_op jit(solution)/shard_map/ppermute | solution.py:28
  99.8 9.5 %collective-permute-start.3 = (bf16[1,512,256]{2,1,0:T(8,128)(2,1)}, bf16[1,512,256]{2,1,0:T(8,128)(2,1)}, u32[]{:S(2)}, u32[]{:S(2)}) collective-permute-start(bf16[1,512,256]{2,1,0:T(8,128)(2,1)} %get-tuple-element.20), channel_id=1, source_target_pairs={{0,1},{1,0},{2,3},{3,2},{32,35},{33,34},{34,33},{35,32},{4,5},{5,4... | collective-permute-start | bytes 786440 | tf_op jit(solution)/shard_map/ppermute | solution.py:28
  109.3 16.0 %collective-permute-start.1 = (bf16[2,512,256]{2,1,0:T(8,128)(2,1)S(1)}, bf16[2,512,256]{2,1,0:T(8,128)(2,1)S(1)}, u32[]{:S(2)}, u32[]{:S(2)}) collective-permute-start(bf16[2,512,256]{2,1,0:T(8,128)(2,1)S(1)} %pad_maximum_fusion.8), channel_id=1, source_target_pairs={{0,3},{1,2},{2,1},{3,0},{32,33},{33,32},{34,35},{35,34},{4,7},{5,6... | collective-permute-start | bytes 1572872 | tf_op jit(solution)/shard_map/ppermute | solution.py:28
  113.5 23.1 %copy-start.11 = (bf16[1,512,256]{2,1,0:T(8,128)(2,1)S(1)}, bf16[1,512,256]{2,1,0:T(8,128)(2,1)}, u32[]{:S(2)}) copy-start(bf16[1,512,256]{2,1,0:T(8,128)(2,1)} %copy-done.10) | copy-start | bytes 786436
  113.5 23.1 %collective-permute-start.4 = (bf16[2,512,256]{2,1,0:T(8,128)(2,1)S(1)}, bf16[2,512,256]{2,1,0:T(8,128)(2,1)S(1)}, u32[]{:S(2)}, u32[]{:S(2)}) collective-permute-start(bf16[2,512,256]{2,1,0:T(8,128)(2,1)S(1)} %pad_maximum_fusion.9), channel_id=1, source_target_pairs={{0,3},{1,2},{2,1},{3,0},{32,33},{33,32},{34,35},{35,34},{4,7},{5,6... | collective-permute-start | bytes 1572872 | tf_op jit(solution)/shard_map/ppermute | solution.py:28
  115.2 23.4 %collective-permute-start.16 = (bf16[4,512,256]{2,1,0:T(8,128)(2,1)S(1)}, bf16[4,512,256]{2,1,0:T(8,128)(2,1)S(1)}, u32[]{:S(2)}, u32[]{:S(2)}) collective-permute-start(bf16[4,512,256]{2,1,0:T(8,128)(2,1)S(1)} %get-tuple-element.13), channel_id=1, source_target_pairs={{0,1},{1,0},{2,3},{3,2},{32,35},{33,34},{34,33},{35,32},{4,5},{5,4... | collective-permute-start | bytes 3145736 | tf_op jit(solution)/shard_map/ppermute | solution.py:28
  125.3 16.0 %collective-permute-start.11 = (bf16[4,512,256]{2,1,0:T(8,128)(2,1)S(1)}, bf16[4,512,256]{2,1,0:T(8,128)(2,1)S(1)}, u32[]{:S(2)}, u32[]{:S(2)}) collective-permute-start(bf16[4,512,256]{2,1,0:T(8,128)(2,1)S(1)} %get-tuple-element.14), channel_id=1, source_target_pairs={{0,1},{1,0},{2,3},{3,2},{32,35},{33,34},{34,33},{35,32},{4,5},{5,4... | collective-permute-start | bytes 3145736 | tf_op jit(solution)/shard_map/ppermute | solution.py:28
  137.8 16.5 %collective-permute-start.14 = (bf16[4,512,256]{2,1,0:T(8,128)(2,1)S(1)}, bf16[4,512,256]{2,1,0:T(8,128)(2,1)S(1)}, u32[]{:S(2)}, u32[]{:S(2)}) collective-permute-start(bf16[4,512,256]{2,1,0:T(8,128)(2,1)S(1)} %get-tuple-element.15), channel_id=1, source_target_pairs={{0,4},{4,0},{8,12},{12,8},{32,44},{36,40},{40,36},{44,32},{1,5},{5... | collective-permute-start | bytes 3145736 | tf_op jit(solution)/shard_map/ppermute | solution.py:28
  138.6 38.2 %collective-permute-start.5 = (bf16[4,512,256]{2,1,0:T(8,128)(2,1)S(1)}, bf16[4,512,256]{2,1,0:T(8,128)(2,1)S(1)}, u32[]{:S(2)}, u32[]{:S(2)}) collective-permute-start(bf16[4,512,256]{2,1,0:T(8,128)(2,1)S(1)} %get-tuple-element.16), channel_id=1, source_target_pairs={{0,4},{4,0},{8,12},{12,8},{32,44},{36,40},{40,36},{44,32},{1,5},{5... | collective-permute-start | bytes 3145736 | tf_op jit(solution)/shard_map/ppermute | solution.py:28
  139.9 64.2 %collective-permute-start.19 = (bf16[1536,1024]{1,0:T(8,128)(2,1)}, bf16[1536,1024]{1,0:T(8,128)(2,1)S(1)}, u32[]{:S(2)}, u32[]{:S(2)}) collective-permute-start(bf16[1536,1024]{1,0:T(8,128)(2,1)} %collective-permute-done.18.same), channel_id=1, source_target_pairs={{0,32},{32,0},{1,33},{33,1},{2,34},{34,2},{3,35},{35,3},{4,36},{36... | collective-permute-start | bytes 9437192 | tf_op jit(solution)/shard_map/ppermute | solution.py:192
  141.3 44.2 %collective-permute-start.17 = (bf16[8,512,256]{2,1,0:T(8,128)(2,1)S(1)}, bf16[8,512,256]{2,1,0:T(8,128)(2,1)S(1)}, u32[]{:S(2)}, u32[]{:S(2)}) collective-permute-start(bf16[8,512,256]{2,1,0:T(8,128)(2,1)S(1)} %pad_maximum_fusion.3.y0), channel_id=1, source_target_pairs={{0,3},{1,2},{2,1},{3,0},{32,33},{33,32},{34,35},{35,34},{4,7},{5,6... | collective-permute-start | bytes 6291464 | tf_op jit(solution)/shard_map/ppermute | solution.py:28
  154.3 22.9 %collective-permute-start.20 = (bf16[512,1024]{1,0:T(8,128)(2,1)S(1)}, bf16[512,1024]{1,0:T(8,128)(2,1)S(1)}, u32[]{:S(2)}, u32[]{:S(2)}) collective-permute-start(bf16[512,1024]{1,0:T(8,128)(2,1)S(1)} %slice.23), channel_id=1, source_target_pairs={{0,64},{64,0},{1,65},{65,1},{2,66},{66,2},{3,67},{67,3},{4,68},{68... | collective-permute-start | bytes 3145736 | tf_op jit(solution)/shard_map/ppermute | solution.py:190
  176.8 27.4 %collective-permute-start.15 = (bf16[8,512,256]{2,1,0:T(8,128)(2,1)S(1)}, bf16[8,512,256]{2,1,0:T(8,128)(2,1)}, u32[]{:S(2)}, u32[]{:S(2)}) collective-permute-start(bf16[8,512,256]{2,1,0:T(8,128)(2,1)S(1)} %pad_maximum_fusion.2.x0), channel_id=1, source_target_pairs={{0,12},{4,8},{8,4},{12,0},{32,36},{36,32},{40,44},{44,40},{1,13},{... | collective-permute-start | bytes 6291464 | tf_op jit(solution)/shard_map/ppermute | solution.py:28
  177.2 41.9 %collective-permute-start.12 = (bf16[8,512,256]{2,1,0:T(8,128)(2,1)S(1)}, bf16[8,512,256]{2,1,0:T(8,128)(2,1)}, u32[]{:S(2)}, u32[]{:S(2)}) collective-permute-start(bf16[8,512,256]{2,1,0:T(8,128)(2,1)S(1)} %pad_maximum_fusion.1.y0), channel_id=1, source_target_pairs={{0,3},{1,2},{2,1},{3,0},{32,33},{33,32},{34,35},{35,34},{4,7},{5,6... | collective-permute-start | bytes 6291464 | tf_op jit(solution)/shard_map/ppermute | solution.py:28
  181.8 44.8 %collective-permute-start.6 = (bf16[8,512,256]{2,1,0:T(8,128)(2,1)S(1)}, bf16[8,512,256]{2,1,0:T(8,128)(2,1)}, u32[]{:S(2)}, u32[]{:S(2)}) collective-permute-start(bf16[8,512,256]{2,1,0:T(8,128)(2,1)S(1)} %pad_maximum_fusion.x0), channel_id=1, source_target_pairs={{0,12},{4,8},{8,4},{12,0},{32,36},{36,32},{40,44},{44,40},{1,13},{... | collective-permute-start | bytes 6291464 | tf_op jit(solution)/shard_map/ppermute | solution.py:28
  186.9 32.2 %collective-permute-start.21 = (bf16[512,1024]{1,0:T(8,128)(2,1)S(1)}, bf16[512,1024]{1,0:T(8,128)(2,1)}, u32[]{:S(2)}, u32[]{:S(2)}) collective-permute-start(bf16[512,1024]{1,0:T(8,128)(2,1)S(1)} %collective-permute-done.20.same), channel_id=1, source_target_pairs={{0,32},{32,0},{1,33},{33,1},{2,34},{34,2},{3,35},{35,3},{4,36},{36... | collective-permute-start | bytes 3145736 | tf_op jit(solution)/shard_map/ppermute | solution.py:193
  (14 other events, 101.4 us)
